TPU v7x, 32 devices: a whole 2x2x4 slice. The times are simulated.
32 devices in a mesh: twin: 2 (over x), dp: 16 (over z, y, core).
Axes of the slice: x: 2, y: 2, z: 4, core: 2. Of those that a mesh axis runs over, the one named last changes fastest.
Arguments:
- hidden_in: bfloat16 [2, 32, 512, 768], P('twin', 'dp'), may hold values from -6 to 6
- seq_lengths: int32 [2, 32], P('twin', 'dp'), may hold values from 64 to 512, as said below
- pos_index: int32 [2, 16, 6], replicated, may hold values from 0 to 15
- pos_count: int32 [2, 16], replicated, may hold values from 1 to 6, as said below
- query_proj: float32 [768, 768], P(('twin', 'dp')), may hold values from -0.21875 to 0.21875
- key_proj: float32 [768, 768], P(('twin', 'dp')), may hold values from -0.21875 to 0.21875
- value_proj: float32 [768, 768], P(('twin', 'dp')), may hold values from -0.21875 to 0.21875
- mixer_proj: float32 [768, 768], P(('twin', 'dp')), may hold values from -3 to 3
- expand_proj: float32 [768, 3072], P(('twin', 'dp')), may hold values from -0.21875 to 0.21875
- shrink_proj: float32 [3072, 768], P(('twin', 'dp')), may hold values from -0.109375 to 0.109375
- query_bias: float32 [768], P(('twin', 'dp')), may hold values from -1 to 1
- value_bias: float32 [768], P(('twin', 'dp')), may hold values from -1 to 1
- mixer_bias: float32 [768], P(('twin', 'dp')), may hold values from -1 to 1
- first_gain: float32 [768], P(('twin', 'dp')), may hold values from 0.5 to 1.5
- first_shift: float32 [768], P(('twin', 'dp')), may hold values from -1 to 1
- expand_bias: float32 [3072], P(('twin', 'dp')), may hold values from -1 to 1
- shrink_bias: float32 [768], P(('twin', 'dp')), may hold values from -1 to 1
- second_gain: float32 [768], P(('twin', 'dp')), may hold values from 0.5 to 1.5
- second_shift: float32 [768], P(('twin', 'dp')), may hold values from -0.3 to 0.3
Outputs:
- loss_value: float32 [], replicated
- hidden_grad: float32 [2, 32, 512, 768], P('twin', 'dp')
- queryproj_grad: float32 [768, 768], P(('twin', 'dp'))
- keyproj_grad: float32 [768, 768], P(('twin', 'dp'))
- valueproj_grad: float32 [768, 768], P(('twin', 'dp'))
- mixerproj_grad: float32 [768, 768], P(('twin', 'dp'))
- expandproj_grad: float32 [768, 3072], P(('twin', 'dp'))
- shrinkproj_grad: float32 [3072, 768], P(('twin', 'dp'))
- querybias_grad: float32 [768], P(('twin', 'dp'))
- valuebias_grad: float32 [768], P(('twin', 'dp'))
- mixerbias_grad: float32 [768], P(('twin', 'dp'))
- firstgain_grad: float32 [768], P(('twin', 'dp'))
- firstshift_grad: float32 [768], P(('twin', 'dp'))
- expandbias_grad: float32 [3072], P(('twin', 'dp'))
- shrinkbias_grad: float32 [768], P(('twin', 'dp'))
- secondgain_grad: float32 [768], P(('twin', 'dp'))
- secondshift_grad: float32 [768], P(('twin', 'dp'))
Inputs may be any that keep to these rules, and one draw needn't show every extreme that they name: `seq_lengths`: each sentence's valid tokens come first; some sentence has 512 and some has 64. Only the first pos_count entries of an anchor's list count; counts are heavy-tailed and both ends occur in every micro-batch. `pos_index`: a list may name a paraphrase more than once; each naming counts.
All inputs are finite; a program needn't handle non-finite values.
Results may differ from a plain program's by a relative error of at most 0.014.
Values may be sent and summed in bfloat16 or wider, within the bound.
A program may use at most 192 MiB of HBM per device.

v0:
```python
import jax
import jax.numpy as jnp
from jax import lax
from jax.experimental import pallas as pl
from jax.experimental.pallas import tpu as pltpu
from jax.sharding import PartitionSpec as P

HEADS = 12
HDIM = 64
MICRO = 2


norm_eps = 1e-12
cosine_scale = 50.0
static_scale = 256.0


def layer_norm(values, gain_vec, shift_vec):
    center = values - jnp.mean(values, axis=-1, keepdims=True)
    spread = jnp.mean(center * center, axis=-1, keepdims=True)
    return center * lax.rsqrt(spread + norm_eps) * gain_vec + shift_vec


def exact_gelu(values):
    return jax.nn.gelu(values, approximate=False)


def product(left, right):
    return jnp.dot(left, right, preferred_element_type=jnp.float32)


def product_lt(left, right):
    return lax.dot_general(
        left, right, (((0,), (0,)), ((), ())), preferred_element_type=jnp.float32
    )


def product_rt(left, right):
    return lax.dot_general(
        left, right, (((1,), (1,)), ((), ())), preferred_element_type=jnp.float32
    )


def column_sum(values):
    return jnp.sum(values.astype(jnp.float32), axis=0)


def batch_loss(pooled_all, pos_list, pos_num):
    anchors = pooled_all.shape[0] // 2
    anchor = pooled_all[:anchors]
    positive = pooled_all[anchors:]
    anchor_n = anchor * lax.rsqrt(jnp.sum(anchor * anchor, axis=-1, keepdims=True) + 1e-06)
    positive_n = positive * lax.rsqrt(jnp.sum(positive * positive, axis=-1, keepdims=True) + 1e-06)
    sims = cosine_scale * jnp.dot(anchor_n, positive_n.T, precision=lax.Precision.HIGHEST)
    row_top = jnp.max(sims, axis=-1, keepdims=True)
    log_total = row_top[:, 0] + jnp.log(jnp.sum(jnp.exp(sims - row_top), axis=-1))
    columns = jnp.arange(anchors, dtype=jnp.int32)
    slots = jnp.arange(pos_list.shape[1], dtype=jnp.int32)
    hits = (pos_list[:, :, None] == columns[None, None, :]) & (
        slots[None, :, None] < pos_num[:, None, None]
    )
    target = jnp.sum(hits.astype(jnp.float32), axis=1) / pos_num[:, None].astype(jnp.float32)
    return jnp.sum(log_total - jnp.sum(target * sims, axis=-1))


def fetch_weights(masters):
    return (
        lax.all_gather(masters[0].astype(jnp.bfloat16), ("twin", "dp"), axis=0, tiled=True),
        lax.all_gather(masters[1].astype(jnp.bfloat16), ("twin", "dp"), axis=0, tiled=True),
        lax.all_gather(masters[2].astype(jnp.bfloat16), ("twin", "dp"), axis=0, tiled=True),
        lax.all_gather(masters[3].astype(jnp.bfloat16), ("twin", "dp"), axis=0, tiled=True),
        lax.all_gather(masters[4].astype(jnp.bfloat16), ("twin", "dp"), axis=0, tiled=True),
        lax.all_gather(masters[5].astype(jnp.bfloat16), ("twin", "dp"), axis=0, tiled=True),
        lax.all_gather(masters[6].astype(jnp.bfloat16), ("twin", "dp"), axis=0, tiled=True),
        lax.all_gather(masters[7].astype(jnp.bfloat16), ("twin", "dp"), axis=0, tiled=True),
        lax.all_gather(masters[8].astype(jnp.bfloat16), ("twin", "dp"), axis=0, tiled=True),
        lax.all_gather(masters[9].astype(jnp.bfloat16), ("twin", "dp"), axis=0, tiled=True),
        lax.all_gather(masters[10].astype(jnp.bfloat16), ("twin", "dp"), axis=0, tiled=True),
        lax.all_gather(masters[11].astype(jnp.bfloat16), ("twin", "dp"), axis=0, tiled=True),
        lax.all_gather(masters[12].astype(jnp.bfloat16), ("twin", "dp"), axis=0, tiled=True),
        lax.all_gather(masters[13].astype(jnp.bfloat16), ("twin", "dp"), axis=0, tiled=True),
        lax.all_gather(masters[14].astype(jnp.bfloat16), ("twin", "dp"), axis=0, tiled=True),
    )


def settle_grads(grad_sums):
    return (
        lax.psum_scatter(grad_sums[0], ("twin", "dp"), scatter_dimension=0, tiled=True),
        lax.psum_scatter(grad_sums[1], ("twin", "dp"), scatter_dimension=0, tiled=True),
        lax.psum_scatter(grad_sums[2], ("twin", "dp"), scatter_dimension=0, tiled=True),
        lax.psum_scatter(grad_sums[3], ("twin", "dp"), scatter_dimension=0, tiled=True),
        lax.psum_scatter(grad_sums[4], ("twin", "dp"), scatter_dimension=0, tiled=True),
        lax.psum_scatter(grad_sums[5], ("twin", "dp"), scatter_dimension=0, tiled=True),
        lax.psum_scatter(grad_sums[6], ("twin", "dp"), scatter_dimension=0, tiled=True),
        lax.psum_scatter(grad_sums[7], ("twin", "dp"), scatter_dimension=0, tiled=True),
        lax.psum_scatter(grad_sums[8], ("twin", "dp"), scatter_dimension=0, tiled=True),
        lax.psum_scatter(grad_sums[9], ("twin", "dp"), scatter_dimension=0, tiled=True),
        lax.psum_scatter(grad_sums[10], ("twin", "dp"), scatter_dimension=0, tiled=True),
        lax.psum_scatter(grad_sums[11], ("twin", "dp"), scatter_dimension=0, tiled=True),
        lax.psum_scatter(grad_sums[12], ("twin", "dp"), scatter_dimension=0, tiled=True),
        lax.psum_scatter(grad_sums[13], ("twin", "dp"), scatter_dimension=0, tiled=True),
        lax.psum_scatter(grad_sums[14], ("twin", "dp"), scatter_dimension=0, tiled=True),
    )


def masked_scores(query_heads, key_heads, live_mask):
    raw_scores = jnp.einsum(
        "sqhd,skhd->shqk", query_heads, key_heads, preferred_element_type=jnp.float32
    ) * HDIM ** (-0.5)
    return jnp.where(live_mask[:, None, None, :], raw_scores, -1000000000.0)


def forward(tokens, live_mask, pool_weight, params):
    seq_count, seq_len, width = tokens.shape
    flat = tokens.reshape(seq_count * seq_len, width)
    head_shape = (seq_count, seq_len, HEADS, HDIM)
    query_heads = (product(flat, params[0]) + params[6]).astype(jnp.bfloat16).reshape(head_shape)
    key_heads = product(flat, params[1]).astype(jnp.bfloat16).reshape(head_shape)
    value_heads = (product(flat, params[2]) + params[7]).astype(jnp.bfloat16).reshape(head_shape)
    scores = masked_scores(query_heads, key_heads, live_mask)
    row_top = jnp.max(scores, axis=-1, keepdims=True)
    exp_terms = jnp.exp(scores - row_top)
    row_total = jnp.sum(exp_terms, axis=-1, keepdims=True)
    log_total = row_top + jnp.log(row_total)
    probs_low = (exp_terms / row_total).astype(jnp.bfloat16)
    mixed = jnp.einsum(
        "shqk,skhd->sqhd", probs_low, value_heads, preferred_element_type=jnp.float32
    )
    mixed = mixed.astype(jnp.bfloat16).reshape(seq_count * seq_len, width)
    first = flat.astype(jnp.float32) + (product(mixed, params[3]) + params[8])
    normed = layer_norm(first, params[9], params[10])
    inner = product(normed.astype(jnp.bfloat16), params[4]) + params[11]
    active = exact_gelu(inner).astype(jnp.bfloat16)
    second = normed + (product(active, params[5]) + params[12])
    output = layer_norm(second, params[13], params[14])
    pooled = jnp.sum(
        output.reshape(seq_count, seq_len, width) * pool_weight[:, :, None], axis=1
    ).astype(jnp.bfloat16)
    saved = (
        query_heads,
        key_heads,
        value_heads,
        log_total,
        mixed,
        first,
        normed,
        inner,
        active,
        second,
    )
    return (pooled, saved)


def backward(tokens, live_mask, pool_weight, params, saved, pool_grad):
    query_heads, key_heads, value_heads, log_total, mixed, first, normed, inner, active, second = (
        saved
    )
    seq_count, seq_len, width = tokens.shape
    flat = tokens.reshape(seq_count * seq_len, width)
    head_shape = (seq_count, seq_len, HEADS, HDIM)
    out_grad = (pool_weight[:, :, None] * pool_grad[:, None, :]).reshape(seq_count * seq_len, width)
    unused, second_pull = jax.vjp(
        layer_norm, second, params[13].astype(jnp.float32), params[14].astype(jnp.float32)
    )
    dsecond, dgain_two, dshift_two = second_pull(out_grad)
    dffn = dsecond.astype(jnp.bfloat16)
    dshrink_bias = column_sum(dffn)
    dshrink = product_lt(active, dffn)
    dactive = product_rt(dffn, params[5])
    unused, gelu_pull = jax.vjp(exact_gelu, inner)
    dinner = gelu_pull(dactive)[0].astype(jnp.bfloat16)
    dexpand_bias = column_sum(dinner)
    dexpand = product_lt(normed.astype(jnp.bfloat16), dinner)
    dnormed = dsecond + product_rt(dinner, params[4])
    unused, first_pull = jax.vjp(
        layer_norm, first, params[9].astype(jnp.float32), params[10].astype(jnp.float32)
    )
    dfirst, dgain_one, dshift_one = first_pull(dnormed)
    dbranch = dfirst.astype(jnp.bfloat16)
    dmixer_bias = column_sum(dbranch)
    dmixer = product_lt(mixed, dbranch)
    dmixed = product_rt(dbranch, params[3]).astype(jnp.bfloat16).reshape(head_shape)
    scores = masked_scores(query_heads, key_heads, live_mask)
    probs_full = jnp.exp(scores - log_total)
    probs_low = probs_full.astype(jnp.bfloat16)
    dvalue = jnp.einsum(
        "shqk,sqhd->skhd", probs_low, dmixed, preferred_element_type=jnp.float32
    ).astype(jnp.bfloat16)
    dprobs = jnp.einsum("sqhd,skhd->shqk", dmixed, value_heads, preferred_element_type=jnp.float32)
    row_delta = jnp.sum(probs_full * dprobs, axis=-1, keepdims=True)
    dscores = (probs_full * (dprobs - row_delta)).astype(jnp.bfloat16)
    dquery = (
        jnp.einsum("shqk,skhd->sqhd", dscores, key_heads, preferred_element_type=jnp.float32)
        * HDIM ** (-0.5)
    ).astype(jnp.bfloat16)
    dkey = (
        jnp.einsum("shqk,sqhd->skhd", dscores, query_heads, preferred_element_type=jnp.float32)
        * HDIM ** (-0.5)
    ).astype(jnp.bfloat16)
    dquery = dquery.reshape(seq_count * seq_len, width)
    dkey = dkey.reshape(seq_count * seq_len, width)
    dvalue = dvalue.reshape(seq_count * seq_len, width)
    dtokens = (
        dfirst
        + product_rt(dquery, params[0])
        + product_rt(dkey, params[1])
        + product_rt(dvalue, params[2])
    )
    grad_terms = (
        product_lt(flat, dquery),
        product_lt(flat, dkey),
        product_lt(flat, dvalue),
        dmixer,
        dexpand,
        dshrink,
        column_sum(dquery),
        column_sum(dvalue),
        dmixer_bias,
        dgain_one,
        dshift_one,
        dexpand_bias,
        dshrink_bias,
        dgain_two,
        dshift_two,
    )
    return (dtokens.reshape(seq_count, seq_len, width), grad_terms)


def staged_device(
    hidden_in,
    seq_lengths,
    pos_index,
    pos_count,
    query_proj,
    key_proj,
    value_proj,
    mixer_proj,
    expand_proj,
    shrink_proj,
    query_bias,
    value_bias,
    mixer_bias,
    first_gain,
    first_shift,
    expand_bias,
    shrink_bias,
    second_gain,
    second_shift,
):
    masters = (
        query_proj,
        key_proj,
        value_proj,
        mixer_proj,
        expand_proj,
        shrink_proj,
        query_bias,
        value_bias,
        mixer_bias,
        first_gain,
        first_shift,
        expand_bias,
        shrink_bias,
        second_gain,
        second_shift,
    )
    tower = lax.axis_index("twin")
    rank = lax.axis_index("dp")
    tokens_all = hidden_in[0]
    lengths_all = seq_lengths[0]
    per_micro = tokens_all.shape[0] // MICRO
    anchors = per_micro * lax.axis_size("dp")
    seq_len = tokens_all.shape[1]
    positions = jnp.arange(seq_len, dtype=jnp.int32)
    own_start = tower * anchors + rank * per_micro
    grad_total = None
    loss_total = jnp.zeros((), jnp.float32)
    input_grads = []
    for micro_step in range(MICRO):
        params = fetch_weights(masters)
        tokens = tokens_all[micro_step * per_micro : (micro_step + 1) * per_micro]
        lengths = lengths_all[micro_step * per_micro : (micro_step + 1) * per_micro]
        live_mask = positions[None, :] < lengths[:, None]
        pool_weight = live_mask.astype(jnp.float32) / lengths[:, None].astype(jnp.float32)
        pooled, saved = forward(tokens, live_mask, pool_weight, params)
        gathered = lax.all_gather(pooled, ("twin", "dp"), axis=0, tiled=True).astype(jnp.float32)
        pos_list = pos_index[micro_step]
        pos_num = pos_count[micro_step]
        loss_part, loss_pull = jax.vjp(
            lambda values: batch_loss(values, pos_list, pos_num), gathered
        )
        gathered_grad = loss_pull(jnp.ones((), jnp.float32))[0] * static_scale
        pool_grad = lax.dynamic_slice_in_dim(gathered_grad, own_start, per_micro, 0)
        dtokens, grad_terms = backward(tokens, live_mask, pool_weight, params, saved, pool_grad)
        input_grads.append(dtokens)
        loss_total = loss_total + loss_part
        grad_total = (
            grad_terms
            if grad_total is None
            else tuple((left + right for left, right in zip(grad_total, grad_terms)))
        )
    shards = settle_grads(grad_total)
    hidden_grad = jnp.concatenate(input_grads, axis=0)[None]
    loss_value = loss_total / (MICRO * anchors)
    return (
        loss_value,
        hidden_grad,
        shards[0],
        shards[1],
        shards[2],
        shards[3],
        shards[4],
        shards[5],
        shards[6],
        shards[7],
        shards[8],
        shards[9],
        shards[10],
        shards[11],
        shards[12],
        shards[13],
        shards[14],
    )


BF = jnp.bfloat16
F32 = jnp.float32
MESH = pl.DeviceIdType.MESH
VMEM_ALL = 67043328
TOK, WIDTH, INNER, SENT = 1024, 768, 3072, 512
SLOTS = 7
QB, VB, MB, G1, S1, EB, SB, G2, S2 = range(9)
VECTOR_SIZES = (24, 24, 24, 24, 24, 96, 24, 24, 24)
PIECES = (
    [(3, 16, 0, 128)]
    + [(0, 24, 0, 384), (0, 24, 384, 384)]
    + [(0, 24, 768 * j, 768) for j in range(1, 4)]
    + [(1, 24, 768 * j, 768) for j in range(4)]
    + [(2, 96, 256 * j, 256) for j in range(3)]
)
GRADS = (
    [(96, 24 * j, 0, 768) for j in range(4)]
    + [(24, 768 * j, 0, 768) for j in range(4)]
    + [(24, 0, 0, 768), (24, 768, 0, 768), (24, 1536, 0, 768)]
    + [(24, 2304, 0, 384), (24, 2304, 384, 384)]
)
VEC = len(GRADS)

AHEAD = 5
FORWARD = {'attend0': {0: ('g2', 'k5', 'a10'), 1: ('f2',), 2: ('g3',), 3: ('k7', 'a12')},
 'attend1': {0: ('k8',), 1: ('g4',), 2: ('i6', 'k9', 'f4')},
 'attend2': {0: ('k10',), 1: ('g5',), 3: ('f5', 'i8', 'k11', 'g6')},
 'exp0': {0: ('k12',), 1: ('g7',), 4: ('f7',), 5: ('i10',)},
 'exp1': {1: ('g8',), 4: ('f8',), 5: ('i11',)},
 'exp2': {1: ('g9',), 4: ('f9',), 5: ('i12',)},
 'exp3': {2: ('g10',), 5: ('f10', 'g11')},
 'mix': {3: ('f6', 'i9')},
 'proj0': {-1: ('f1',), 1: ('i3',)},
 'proj1': {-1: ('f3',), 2: ('i5',)},
 'proj2': {4: ('i7',)},
 'projh': {0: ('i4',), 1: ('k6', 'a11')},
 'shr1': {-1: ('g12', 'f11')},
 'shr2': {-1: ('f12',)},
 'vec': {-1: ('k0',
              'a5',
              'k1',
              'a6',
              'i0',
              'k2',
              'a7',
              'i1',
              'g0',
              'k3',
              'a8',
              'i2',
              'f0'),
         5: ('g1',),
         7: ('k4', 'a9')}}
BACKWARD = {'actb': {2: ('c0', 'r0'),
          3: ('c1', 'r1'),
          4: ('c2', 'r2', 'c3', 'r3'),
          6: ('d0',),
          8: ('d1',),
          10: ('d2',)},
 'attb0': {0: ('c8', 's5', 'r8'), 2: ('f4', 's6'), 3: ('s7', 'f5')},
 'attb1': {1: ('f6', 's8', 'c9', 'r9'), 2: ('f7',), 3: ('d9',)},
 'attb2': {0: ('f8',), 1: ('s9', 'c10', 'r10'), 2: ('c11', 'r11'), 3: ('d10',)},
 'expg0': {0: ('d3',)},
 'expg1': {1: ('s0',)},
 'expg2': {0: ('c4', 'r4'), 2: ('s1', 'c5', 'r5')},
 'expg3': {2: ('s2',)},
 'firstb': {0: ('r6',),
            1: ('f1', 's3', 'd4', 'c7', 'r7'),
            2: ('f2', 'd5', 'd6')},
 'inb': {0: ('c12', 's10', 'r12', 'c13', 'r13'),
         1: ('s11',),
         2: ('d12', 'd13')},
 'ing0': {0: ('d8',)},
 'ingh1': {0: ('f9',), 1: ('d11',)},
 'mixb': {0: ('f3', 'd7')},
 'mixg': {1: ('s4',)},
 'st7': {-1: ('c6', 'f0')},
 'tail': {-1: ('f10', 's12', 's13', 'f11', 'f12', 'f13')}}


def coords():
    rank = lax.axis_index("dp")
    return lax.axis_index("twin"), rank // 4, (rank // 2) % 2, rank % 2


def flat(t, z, y, c):
    return t * 16 + z * 4 + y * 2 + c


def dev(t, z, y, c):
    return {"twin": t, "dp": z * 4 + y * 2 + c}


def neighbours(t, z, y, c):
    return [dev(t, (z + k) % 4, y, c) for k in (1, 2, 3)] + [
        dev(1 - t, z, y, c),
        dev(t, z, 1 - y, c),
        dev(t, z, y, 1 - c),
    ]


def signal_all(sem):
    for other in neighbours(*coords()):
        pl.semaphore_signal(sem, inc=1, device_id=other, device_id_type=MESH)


def send(src, dst, send_sem, recv_sem, target):
    pltpu.make_async_remote_copy(
        src, dst, send_sem, recv_sem, device_id=target, device_id_type=MESH
    ).start()


def wait_bytes(ref, sem):
    pltpu.make_async_copy(ref, ref, sem).wait()


class Gather:
    def __init__(self, arrays, recv, sent):
        self.arrays, self.recv, self.sent = arrays, recv, sent
        self.at = coords()

    def rows(self, p, owner):
        w, r, c0, nc = PIECES[p]
        return self.arrays[w].at[pl.ds(pl.multiple_of(owner * r, 8), r), pl.ds(c0, nc)]

    def halves(self, p, owners, half):
        w, r, c0, nc = PIECES[p]
        if nc % 256:
            return [self.rows(p, owner) for owner in owners[2 * half : 2 * half + 2]]
        cols = pl.ds(c0 + half * (nc // 2), nc // 2)
        return [
            self.arrays[w].at[pl.ds(pl.multiple_of(owner * r, 8), r), cols] for owner in owners
        ]

    def put(self, p, part, target, group):
        send(part, part, self.sent.at[p], self.recv.at[p, group], target)

    def wait(self, p, group, shards):
        w, r, c0, nc = PIECES[p]
        wait_bytes(
            self.arrays[w].at[pl.ds(0, shards * r), pl.ds(c0, nc)], self.recv.at[p, group]
        )

    def start(self, p):
        t, z, y, c = self.at
        own = self.rows(p, flat(t, z, y, c))
        for k in (1, 2, 3):
            self.put(p, own, dev(t, (z + k) % 4, y, c), 0)
        self.put(p, own, dev(1 - t, z, y, c), 1)
        self.put(p, own, dev(t, z, 1 - y, c), 2)
        self.put(p, own, dev(t, z, y, 1 - c), 5)

    def column(self, p):
        t, z, y, c = self.at
        self.wait(p, 0, 3)
        for k in (1, 2, 3):
            part = self.rows(p, flat(t, (z + k) % 4, y, c))
            self.put(p, part, dev(1 - t, z, y, c), 1)
            self.put(p, part, dev(t, z, 1 - y, c), 2)
            self.put(p, part, dev(t, z, y, 1 - c), 5)

    def sides(self, p):
        t, z, y, c = self.at
        self.wait(p, 1, 4)
        owners = [flat(1 - t, k, y, c) for k in range(4)]
        for part in self.halves(p, owners, 0):
            self.put(p, part, dev(t, z, 1 - y, c), 4)
        for owner in owners:
            self.put(p, self.rows(p, owner), dev(t, z, y, 1 - c), 5)
        self.wait(p, 2, 4)
        owners = [flat(t, k, 1 - y, c) for k in range(4)]
        for part in self.halves(p, owners, 1):
            self.put(p, part, dev(1 - t, z, y, c), 3)
        for owner in owners:
            self.put(p, self.rows(p, owner), dev(t, z, y, 1 - c), 5)

    def diagonal(self, p):
        t, z, y, c = self.at
        owners = [flat(1 - t, k, 1 - y, c) for k in range(4)]
        for group, half in ((3, 1), (4, 0)):
            self.wait(p, group, 2)
            for part in self.halves(p, owners, half):
                self.put(p, part, dev(t, z, y, 1 - c), 5)

    def finish(self, p):
        self.wait(p, 5, 16)

    def drain(self, p):
        w, r, c0, nc = PIECES[p]
        wait_bytes(self.arrays[w].at[pl.ds(0, 31 * r), pl.ds(c0, nc)], self.sent.at[p])

    def table(self):
        return {
            "a": self.start,
            "k": self.column,
            "i": self.sides,
            "g": self.diagonal,
            "f": self.finish,
        }


class Scatter:
    def __init__(self, grad, bufs, vec_grad, vec_bufs, recv, sent, free, store):
        self.grad, self.bufs, self.vec_grad, self.vec_bufs = grad, bufs, vec_grad, vec_bufs
        self.recv, self.sent, self.free, self.store = recv, sent, free, store
        self.at = coords()

    def size(self, p):
        return (16, 128) if p == VEC else (24, GRADS[p][3])

    def buf(self, p, which):
        if p == VEC:
            return self.vec_bufs[which]
        whole = self.bufs[which].at[p % SLOTS]
        if GRADS[p][3] == 768:
            return whole
        cols = pl.ds(0, 384)
        if which == 0:
            return whole.at[:, cols]
        if which == 1:
            return whole.at[:, pl.ds(0, 48), :]
        return whole.at[:, :, cols]

    def part(self, p, owner):
        if p == VEC:
            return self.vec_grad.at[pl.ds(pl.multiple_of(owner * 16, 8), 16), :]
        stride, base, col, cols = GRADS[p]
        return self.grad.at[
            pl.ds(pl.multiple_of(owner * stride + base, 8), 24), pl.ds(col, cols)
        ]

    def mine(self, p, t, z, y, n=1):
        r, nc = self.size(p)
        first = pl.multiple_of((t * 8 + y * 4 + z) * r, 8)
        return self.buf(p, 0).at[pl.ds(first, n * r), :]

    def half(self, p, t, y, half):
        r, nc = self.size(p)
        first = (t * 8 + y * 4) * r
        if nc < 768:
            first = pl.multiple_of(first + half * 2 * r, 8)
            return self.buf(p, 0).at[pl.ds(first, 2 * r), :]
        return self.buf(p, 0).at[
            pl.ds(pl.multiple_of(first, 8), 4 * r), pl.ds(half * (nc // 2), nc // 2)
        ]

    def put(self, p, group, src, dst, target, lane=1):
        send(src, dst, self.sent.at[p, lane], self.recv.at[p, group], target)

    def start(self, p):
        t, z, y, c = self.at
        if SLOTS <= p < VEC:
            pl.semaphore_wait(self.free.at[p % SLOTS], 6)

        def body(i, carry):
            tt, yy, zz = i // 8, (i // 4) % 2, i % 4
            src = self.part(p, flat(tt, zz, yy, 1 - c))
            self.put(p, 0, src, self.mine(p, tt, zz, yy), dev(t, z, y, 1 - c), 0)
            return carry

        lax.fori_loop(0, 16, body, 0)

    def add_columns(self, p, first, last):
        t, z, y, c = self.at

        def body(i, carry):
            tt = (t + 1 - i // 8) % 2
            yy = (y + 1 - (i // 4) % 2) % 2
            a = self.mine(p, tt, i % 4, yy)
            b = self.part(p, flat(tt, i % 4, yy, c))
            a[...] = a[...] + b[...]
            return carry

        lax.fori_loop(first, last, body, 0)

    def cores(self, p):
        t, z, y, c = self.at
        wait_bytes(self.buf(p, 0), self.recv.at[p, 0])
        self.add_columns(p, 0, 4)
        diag = self.buf(p, 1)
        self.put(p, 2, self.half(p, 1 - t, 1 - y, 0), diag.at[0], dev(t, z, 1 - y, c))
        self.put(p, 1, self.half(p, 1 - t, 1 - y, 1), diag.at[1], dev(1 - t, z, y, c))
        self.add_columns(p, 4, 16)

    def add(self, a, b):
        a[...] = a[...] + b[...]

    def diagonals(self, p):
        t, z, y, c = self.at
        diag, side = self.buf(p, 1), self.buf(p, 2)
        wait_bytes(diag.at[0], self.recv.at[p, 2])
        self.add(self.half(p, 1 - t, y, 0), diag.at[0])
        self.put(p, 3, self.mine(p, 1 - t, 0, y, 4), side.at[0], dev(1 - t, z, y, c))
        wait_bytes(diag.at[1], self.recv.at[p, 1])
        self.add(self.half(p, t, 1 - y, 1), diag.at[1])
        self.put(p, 4, self.mine(p, t, 0, 1 - y, 4), side.at[1], dev(t, z, 1 - y, c))

    def sides(self, p):
        t, z, y, c = self.at
        side, col = self.buf(p, 2), self.buf(p, 3)
        wait_bytes(side.at[0], self.recv.at[p, 3])
        wait_bytes(side.at[1], self.recv.at[p, 4])
        a = self.mine(p, t, 0, y, 4)
        total = a[...].astype(F32) + side[0].astype(F32) + side[1].astype(F32)
        a[...] = total.astype(a.dtype)
        for k in (1, 2, 3):
            zz = (z + k) % 4
            self.put(p, 5, self.mine(p, t, zz, y), col.at[k - 1], dev(t, zz, y, c))

    def finish(self, p):
        t, z, y, c = self.at
        col = self.buf(p, 3)
        wait_bytes(col, self.recv.at[p, 5])
        total = self.mine(p, t, z, y)[...].astype(F32)
        for k in range(3):
            total = total + col[k].astype(F32)
        self.store(p, total)
        self.drain(p)
        if p + SLOTS < VEC:
            signal_all(self.free.at[p])

    def drain(self, p):
        r, nc = self.size(p)
        wait_bytes(self.buf(p, 0).at[pl.ds(0, 15 * r), :], self.sent.at[p, 1])

    def table(self):
        return {
            "c": self.cores,
            "d": self.diagonals,
            "s": self.sides,
            "f": self.finish,
            "r": self.release,
        }

    def release(self, p):
        wait_bytes(self.buf(p, 0), self.sent.at[p, 0])


def dot(a, b):
    return jnp.dot(a, b, preferred_element_type=F32)


def dot_lt(a, b):
    return lax.dot_general(a, b, (((0,), (0,)), ((), ())), preferred_element_type=F32)


def dot_rt(a, b):
    return lax.dot_general(a, b, (((1,), (1,)), ((), ())), preferred_element_type=F32)


def block(i, n):
    return pl.ds(pl.multiple_of(i * n, n), n)


def iota(shape, axis):
    return lax.broadcasted_iota(jnp.int32, shape, axis)


def loop(n, body, ticks=()):
    ticks = {k: v for k, v in dict(ticks).items() if k >= 0}

    def step(i, carry):
        body(i)
        for k, tick in ticks.items():

            @pl.when(i == k)
            def _(tick=tick):
                for part in tick:
                    part()

        return carry

    lax.fori_loop(0, n, step, 0)


def ticks_of(plan, name, table):
    return {
        k: [lambda n=n: table[n[0]](int(n[1:])) for n in names]
        for k, names in plan.get(name, {}).items()
    }


def owner_of(n, size):
    owner = jnp.floor((n.astype(F32) + 0.5) * (1.0 / size)).astype(jnp.int32)
    return owner, n - owner * size


def vector_row(vec, k):
    size = VECTOR_SIZES[k]
    width = 32 * size
    owner, place = owner_of(iota((1, width), 1), size)
    shards = vec[pl.ds(k, 32, stride=16), :].astype(BF)
    pick = jnp.where(iota((128, width), 0) == place, 1.0, 0.0).astype(BF)
    spreaded = dot(shards, pick)
    return jnp.sum(jnp.where(iota((32, width), 0) == owner, spreaded, 0.0), axis=0, keepdims=True)


def vector_tiles(row, k):
    size = VECTOR_SIZES[k]
    width = 32 * size
    owner, place = owner_of(iota((1, width), 1), size)
    pick = jnp.where(iota((128, width), 0) == place, 1.0, 0.0)
    parts = jnp.where(iota((32, width), 0) == owner, row, 0.0)
    return lax.dot_general(
        parts,
        pick,
        (((1,), (1,)), ((), ())),
        precision=lax.Precision.HIGHEST,
        preferred_element_type=F32,
    )


def normalize(v):
    center = v - jnp.mean(v, axis=1, keepdims=True)
    spread_ = jnp.mean(center * center, axis=1, keepdims=True)
    scale = lax.rsqrt(spread_ + norm_eps)
    return center * scale, scale


def contrast(pool, pos, cnt, dpool, own):
    total = jnp.zeros((1, 1), F32)
    row, col = iota((32, 32), 0), iota((32, 32), 1)
    valid = (row < 16) & (col >= 16)
    eye = row == col
    for m in range(MICRO):
        chunks = [pool[pl.ds(8 * m + k, 32, stride=16), :] for k in range(6)]
        gram = jnp.zeros((32, 32), F32)
        for chunk in chunks:
            gram = gram + dot_rt(chunk.astype(BF), chunk.astype(BF))
        diag = jnp.where(eye, gram, 0.0)
        scale_c = lax.rsqrt(jnp.sum(diag, axis=1, keepdims=True) + 1e-6)
        scale_r = lax.rsqrt(jnp.sum(diag, axis=0, keepdims=True) + 1e-6)
        sims = cosine_scale * gram * scale_c * scale_r
        top = jnp.max(jnp.where(valid, sims, -1e30), axis=1, keepdims=True)
        terms = jnp.where(valid, jnp.exp(jnp.minimum(sims - top, 0.0)), 0.0)
        row_sum = jnp.where(row[:, :1] < 16, jnp.sum(terms, axis=1, keepdims=True), 1.0)
        logs = jnp.where(row[:, :1] < 16, top + jnp.log(row_sum), 0.0)
        hits = jnp.zeros((16, 32), F32)
        eye16 = iota((16, 16), 0) == iota((16, 16), 1)
        number = jnp.sum(jnp.where(eye16, cnt[m : m + 1, :], 0), axis=1, keepdims=True)
        for k in range(6):
            hit = (pos[m, :, k : k + 1] + 16 == iota((16, 32), 1)) & (k < number)
            hits = hits + jnp.where(hit, 1.0, 0.0)
        target = jnp.concatenate([hits / number.astype(F32), jnp.zeros((16, 32), F32)], axis=0)
        loss = logs - jnp.sum(target * sims, axis=1, keepdims=True)
        total = total + jnp.sum(jnp.where(row[:, :1] < 16, loss, 0.0), axis=0, keepdims=True)
        grad = (terms / row_sum - target) * static_scale
        mine_r = jnp.sum(jnp.where(row == own, grad * scale_r, 0.0), axis=0, keepdims=True)
        weight = jnp.sum(jnp.where(eye, mine_r, 0.0), axis=1, keepdims=True)
        weight = weight + jnp.sum(
            jnp.where(col == own, grad * scale_c, 0.0), axis=1, keepdims=True
        )
        weight = cosine_scale * weight
        mine = iota((32, 1), 0) == own
        scale = jnp.sum(jnp.where(mine, scale_c, 0.0), axis=0, keepdims=True)
        along = jnp.zeros((1, 1), F32)
        pulls = []
        for chunk in chunks:
            pull = jnp.sum(weight * chunk, axis=0, keepdims=True)
            x = jnp.sum(jnp.where(mine, chunk, 0.0), axis=0, keepdims=True)
            along = along + jnp.sum(pull * x, axis=1, keepdims=True)
            pulls.append((pull, x))
        for k, (pull, x) in enumerate(pulls):
            dpool[m : m + 1, 128 * k : 128 * k + 128] = scale * pull - x * (
                scale * scale * scale * along
            )
    return total


def step_kernel(*refs):
    (lens, tokens, pos, cnt, mq, mk, mv, mm, me, ms) = refs[:10]
    mvec = refs[10:19]
    (loss, hidden, probs, gq, gk, gv, gm, ge, gs, gvec) = refs[19:29]
    (wa, we, ws, vec, grad, rc, rd, rs, rz, act, gp, qkv, mixed, nb, n1, n2) = refs[29:45]
    (f1, pbuf, r1, r2, par, pgrad, nbar, dpool, pool, poolf) = refs[45:55]
    (vc, vd, vs, vz) = refs[55:59]
    vgrad = vec
    (g_recv, g_sent, s_recv, s_sent, free, pool_recv, pool_sent, p_sem, h_sem, in_sem, x) = refs[59:]
    t, z, y, c = coords()
    own = flat(t, z, y, c)
    gather = Gather((wa, we, ws, vec), g_recv, g_sent)

    rows = (0, 24, 48, 72, 192, 216, 240, 264, 96)
    wide = [me.at[:, pl.ds(768 * j, 768)] for j in range(4)]
    loads = [
        pltpu.make_async_copy(shard, f1.at[pl.ds(row, shard.shape[0]), :], in_sem.at[k])
        for k, (row, shard) in enumerate(zip(rows, [mq, mk, mv, mm, *wide, ms]))
    ]
    loads.append(pltpu.make_async_copy(tokens, x, in_sem.at[9]))
    for load in loads:
        load.start()
    barrier = pltpu.get_barrier_semaphore()
    signal_all(barrier)
    here24 = pl.ds(pl.multiple_of(own * 24, 8), 24)
    here16 = pl.ds(pl.multiple_of(own * 16, 8), 16)
    vec[here16, :] = jnp.zeros((16, 128), F32)
    for k, size in enumerate(VECTOR_SIZES):
        vec[pl.ds(own * 16 + k, 1), 0:size] = (
            mvec[k][...].reshape(1, size).astype(BF).astype(F32)
        )
    pl.semaphore_wait(barrier, 6)
    gather.start(0)
    for load in loads[:3]:
        load.wait()
    for g in range(6):
        for j in range(3):
            first = 384 * g + 128 * j
            shard = f1[24 * j : 24 * j + 24, 128 * g : 128 * g + 128]
            wa[here24, first : first + 128] = shard.astype(BF)
        if g in (0, 1, 3, 5):
            gather.start((g + 3) // 2 if g else 1)
    for load in loads[3:9]:
        load.wait()
    wa[here24, 2304:3072] = f1[72:96, :].astype(BF)
    for j in range(4):
        we[here24, 768 * j : 768 * j + 768] = f1[192 + 24 * j : 216 + 24 * j, :].astype(BF)
    ws[pl.ds(pl.multiple_of(own * 96, 8), 96), :] = f1[96:192, :].astype(BF)

    def planned(name):
        ticks = ticks_of(FORWARD, name, gather.table())
        for part in ticks.get(-1, ()):
            part()
        return ticks

    ticks = planned("vec")
    for k, size in enumerate(VECTOR_SIZES):
        par[k : k + 1, 0 : 32 * size] = vector_row(vec, k)
        for part in ticks.get(k, ()):
            part()

    for g in range(6):
        lanes, first = slice(128 * g, 128 * g + 128), 384 * g
        par[9:10, first : first + 128] = par[QB : QB + 1, lanes] * HDIM ** (-0.5)
        par[9:10, first + 128 : first + 256] = jnp.zeros((1, 128), F32)
        par[9:10, first + 256 : first + 384] = par[VB : VB + 1, lanes]
        par[10:11, first : first + 128] = jnp.full((1, 128), HDIM ** (-0.5), F32)
        par[10:11, first + 128 : first + 384] = jnp.ones((1, 256), F32)
    loads[9].wait()

    first_head = iota((SENT, 128), 1) < 64

    def put_probs(slot, item):
        return pltpu.make_async_copy(pbuf.at[slot], probs.at[item], p_sem.at[slot])

    def project(first, size, blocks):
        def body(i):
            rows = block(i // blocks, 512)
            cols = pl.ds(pl.multiple_of(first + i % blocks * size, 128), size)
            value = dot(x[rows, :], wa[:, cols])
            qkv[rows, cols] = (value * par[10:11, cols] + par[9:10, cols]).astype(BF)

        return body

    def second_half():
        loop(2, project(384, 384, 1), planned("projh"))

    def triple(pair):
        return [pl.ds(pl.multiple_of(384 * pair + 128 * n, 128), 128) for n in range(3)]

    def attend(g):
        def body(i):
            item = 4 * g + i
            s, j = i % 2, i // 2
            slot = item % 2
            rows = block(s, SENT)
            live = iota((1, SENT), 1) < lens[s]
            if g:
                put_probs(slot, item - 2).wait()
            else:

                @pl.when(i >= 2)
                def _():
                    put_probs(slot, item - 2).wait()

            q, k, v = [qkv[rows, cols] for cols in triple(2 * g + j)]
            zero = jnp.zeros_like(q)
            outs = []
            for h in range(2):
                qh = jnp.where(first_head if h == 0 else ~first_head, q, zero)
                scores = jnp.where(live, dot_rt(qh, k), -1000000000.0)
                terms = jnp.exp(scores - jnp.max(scores, axis=1, keepdims=True))
                low = (terms * (1.0 / jnp.sum(terms, axis=1, keepdims=True))).astype(BF)
                pbuf[slot, h] = low
                outs.append(dot(low, v))
            mixed[rows, block(2 * g + j, 128)] = jnp.where(first_head, outs[0], outs[1]).astype(BF)
            put_probs(slot, item).start()

        return body

    for g in range(3):
        if g == 0:
            loop(2, project(0, 384, 1), planned("proj0"))
        else:
            loop(6, project(768 * g, 256, 3), planned("proj%d" % g))
        ticks = planned("attend%d" % g)
        if g == 0:
            ticks.setdefault(1, []).append(second_half)
        loop(4, attend(g), ticks)
    for item in (10, 11):
        put_probs(item % 2, item).wait()

    def mix(i):
        rows = block(i, 256)
        first = dot(mixed[rows, :], wa[:, 2304:3072]) + par[MB : MB + 1, 0:768]
        n, r = normalize(x[rows, :].astype(F32) + first)
        n1[rows, :] = n.astype(BF)
        r1[rows, :] = r
        normed = n * par[G1 : G1 + 1, 0:768] + par[S1 : S1 + 1, 0:768]
        f1[rows, :] = normed
        nb[rows, :] = normed.astype(BF)

    loop(4, mix, planned("mix"))

    for j in range(4):

        def expand(i, j=j):
            rows, cols = block(i % 2, 512), block(3 * j + i // 2, 256)
            v = dot(nb[rows, :], we[:, cols]) + par[EB : EB + 1, cols]
            phi = 0.5 + 0.5 * lax.erf(v * 0.7071067811865476)
            act[rows, cols] = (v * phi).astype(BF)
            slope = phi + v * (jnp.exp(-0.5 * (v * v)) * 0.3989422804014327)
            gp[rows, cols] = slope.astype(BF)

        loop(6, expand, planned("exp%d" % j))
    for j in range(3):

        def shrink(i, j=j):
            rows, cols = block(i, 512), slice(256 * j, 256 * j + 256)
            value = dot(act[rows, :], ws[:, cols]) + par[SB : SB + 1, cols]
            f1[rows, cols] = f1[rows, cols] + value

        loop(2, shrink, planned("shr%d" % j))

    nbar[...] = jnp.zeros_like(nbar)

    def weight_of(i, n):
        s = (i * n) // SENT
        length = lens[s]
        token = iota((n, 1), 0) + (i * n - s * SENT)
        return jnp.where(token < length, 1.0, 0.0) / length.astype(F32)

    def finish_norm(i):
        rows = block(i, 128)
        n, r = normalize(f1[rows, :])
        w = weight_of(i, 128)
        n2[rows, :] = n.astype(BF)
        r2[rows, :] = r * w
        total = jnp.sum(n * w, axis=0, keepdims=True)
        s = i // 4
        nbar[pl.ds(s, 1), :] = nbar[pl.ds(s, 1), :] + total

    loop(8, finish_norm)
    pooled = nbar[0:2, :] * par[G2 : G2 + 1, 0:768] + par[S2 : S2 + 1, 0:768]
    tile = jnp.zeros((16, 128), F32)
    place = iota((16, 128), 0)
    for m in range(2):
        for k in range(6):
            tile = jnp.where(place == 8 * m + k, pooled[m : m + 1, 128 * k : 128 * k + 128], tile)
    at = pool.at[pl.ds(pl.multiple_of(own * 16, 8), 16), :]
    at[...] = tile.astype(BF)

    def spread_pool(i, carry):
        other = lax.rem(own + i, 32)
        target = {"twin": other // 16, "dp": lax.rem(other, 16)}
        send(at, at, pool_sent, pool_recv, target)
        return carry

    lax.fori_loop(1, 32, spread_pool, 0)
    for p in range(len(PIECES)):
        gather.drain(p)
    wait_bytes(pool.at[pl.ds(0, 496), :], pool_recv)
    poolf[...] = pool[...].astype(F32)
    loss[...] = contrast(poolf, pos, cnt, dpool, own) / (MICRO * 16)
    wait_bytes(pool.at[pl.ds(0, 496), :], pool_sent)

    def store(p, total):
        if p == VEC:
            gvec[...] = total
        elif p < 4:
            gs[24 * p : 24 * p + 24, :] = total
        elif p < 8:
            ge[:, 768 * (p - 4) : 768 * (p - 4) + 768] = total
        elif p == 8:
            gm[...] = total
        else:
            for j in range(total.shape[1] // 384):
                pair = 2 * (p - 9) + j if p < 11 else p - 7
                for n, ref in enumerate((gq, gk, gv)):
                    first = 384 * j + 128 * n
                    ref[:, 128 * pair : 128 * pair + 128] = total[:, first : first + 128]

    scatter = Scatter(
        grad, (rc, rd, rs, rz), vgrad, (vc, vd, vs, vz), s_recv, s_sent, free, store
    )
    pgrad[...] = jnp.zeros_like(pgrad)
    gain2 = par[G2 : G2 + 1, 0:768]
    pgrad[G2 : G2 + 1, 0:768] = jnp.sum(dpool[0:2, :] * nbar[0:2, :], axis=0, keepdims=True)
    pgrad[S2 : S2 + 1, 0:768] = jnp.sum(dpool[0:2, :], axis=0, keepdims=True)

    def collect(k, value):
        cols = slice(0, 32 * VECTOR_SIZES[k])
        pgrad[k : k + 1, cols] = pgrad[k : k + 1, cols] + jnp.sum(value, axis=0, keepdims=True)

    def second_back(i):
        rows = block(i, 128)
        u = dpool[pl.ds(i // 4, 1), :] * gain2
        u = u - jnp.mean(u, axis=1, keepdims=True)
        n = n2[rows, :].astype(F32)
        along = jnp.mean(n * u, axis=1, keepdims=True)
        back = r2[rows, :] * (u - n * along)
        f1[rows, :] = back
        low = back.astype(BF)
        n2[rows, :] = low
        collect(SB, low.astype(F32))

    loop(8, second_back)

    def shrink_grad(i):
        grad[block(i, 256), :] = dot_lt(act[:, block(i, 256)], n2[...]).astype(BF)

    loop(12, shrink_grad)
    for p in range(4):
        scatter.start(p)

    def planned(name):
        ticks = ticks_of(BACKWARD, name, scatter.table())
        for part in ticks.get(-1, ()):
            part()
        return ticks

    def act_back(i):
        cols = block(i, 256)
        back = dot_rt(n2[...], ws[cols, :]) * gp[:, cols].astype(F32)
        low = back.astype(BF)
        gp[:, cols] = low
        pgrad[EB : EB + 1, cols] = jnp.sum(low.astype(F32), axis=0, keepdims=True)

    loop(12, act_back, planned("actb"))
    planned("expg")

    def expand_grad(i, j):
        cols = block(3 * j + i, 256)
        grad[768 * j : 768 * j + 768, block(i, 256)] = dot_lt(nb[...], gp[:, cols]).astype(BF)

    for j in range(4):
        loop(3, lambda i, j=j: expand_grad(i, j), planned("expg%d" % j))
        planned("st%d" % (4 + j))
        scatter.start(4 + j)

    def first_back(i):
        rows = block(i, 256)
        back = f1[rows, :] + dot_rt(gp[rows, :], we[...])
        n = n1[rows, :].astype(F32)
        collect(G1, back * n)
        collect(S1, back)
        dn = back * par[G1 : G1 + 1, 0:768]
        mean = jnp.mean(dn, axis=1, keepdims=True)
        along = jnp.mean(dn * n, axis=1, keepdims=True)
        back = r1[rows, :] * (dn - mean - n * along)
        f1[rows, :] = back
        low = back.astype(BF)
        n2[rows, :] = low
        collect(MB, low.astype(F32))

    loop(4, first_back, planned("firstb"))

    def mixer_grad(i):
        grad[0:768, block(i, 256)] = dot_lt(mixed[...], n2[:, block(i, 256)]).astype(BF)

    loop(3, mixer_grad, planned("mixg"))
    planned("st8")
    scatter.start(8)

    def get_probs(item):
        return pltpu.make_async_copy(probs.at[item], pbuf.at[item % 2], p_sem.at[item % 2])

    get_probs(0).start()
    get_probs(1).start()

    def mixed_back(i):
        rows = block(i, 512)
        n2[rows, :] = dot_rt(n2[rows, :], wa[:, 2304:3072]).astype(BF)

    loop(2, mixed_back, planned("mixb"))
    planned("att")

    for g in range(3):

        def attend_back(i, g=g):
            s, j = i % 2, i // 2
            pair = 2 * g + j
            item = 4 * g + i
            slot = i % 2
            rows = block(s, SENT)
            get_probs(item).wait()
            q, k, v = [qkv[rows, cols] for cols in triple(pair)]
            do = n2[rows, block(pair, 128)]
            zero = jnp.zeros_like(do)
            both = do.astype(F32) * mixed[rows, block(pair, 128)].astype(F32)
            parts = []
            for h in range(2):
                head = first_head if h == 0 else ~first_head
                p = pbuf[slot, h]
                delta = jnp.sum(jnp.where(head, both, 0.0), axis=1, keepdims=True)
                dp = dot_rt(jnp.where(head, do, zero), v)
                ds = (p.astype(F32) * (dp - delta)).astype(BF)
                parts.append((dot(ds, k) * (HDIM ** (-0.5)), dot_lt(ds, q), dot_lt(p, do)))
            for n, cols in enumerate(triple(pair)):
                value = jnp.where(first_head, parts[0][n], parts[1][n])
                act[rows, cols] = value.astype(BF)

            @pl.when(item + 2 < 12)
            def _():
                get_probs(item + 2).start()

        def half_grad(j):
            def body(i):
                cols = pl.ds(1536 + 384 * j, 384)
                grad[pl.ds(pl.multiple_of(2304 + 384 * i, 8), 384), 384 * j : 384 * j + 384] = (
                    dot_lt(x[:, block(i, 384)], act[:, cols]).astype(BF)
                )

            loop(2, body, planned("ingh%d" % j))
            planned("st%d" % (11 + j))
            scatter.start(11 + j)

        def input_grad(i, g=g):
            grad[768 * (g + 1) : 768 * (g + 2), block(i, 256)] = dot_lt(
                x[...], act[:, block(3 * g + i, 256)]
            ).astype(BF)

        ticks = planned("attb%d" % g)
        if g == 2:
            ticks.setdefault(1, []).append(lambda: half_grad(0))
        loop(4, attend_back, ticks)
        if g == 2:
            half_grad(1)
        else:
            loop(3, input_grad, planned("ing%d" % g))
            planned("st%d" % (9 + g))
            scatter.start(9 + g)
        for j in range(2):
            first, lanes = 768 * g + 384 * j, slice(256 * g + 128 * j, 256 * g + 128 * j + 128)
            for k, col in ((QB, first), (VB, first + 256)):
                pgrad[k : k + 1, lanes] = jnp.sum(
                    act[:, col : col + 128].astype(F32), axis=0, keepdims=True
                )
    for k in range(9):
        tiles = vector_tiles(pgrad[k : k + 1, 0 : 32 * VECTOR_SIZES[k]], k)
        vgrad[pl.ds(k, 32, stride=16), :] = tiles
    scatter.start(VEC)

    def put_hidden(i):
        rows = block(i, 256)
        return pltpu.make_async_copy(f1.at[rows, :], hidden.at[rows, :], h_sem.at[i])

    def input_back(i):
        rows = block(i, 256)
        f1[rows, :] = f1[rows, :] + dot_rt(act[rows, 0:2304], wa[:, 0:2304])
        put_hidden(i).start()

    loop(4, input_back, planned("inb"))
    planned("tail")
    for i in range(4):
        put_hidden(i).wait()


def emit_kernel(*refs):
    hidden, shards, gvec, loss = refs[0], refs[1:7], refs[7], refs[8]
    hidden_o, shards_o, vectors_o, loss_o = refs[9], refs[10:16], refs[16:25], refs[25]
    held, parts, sem_in, sem_out = refs[26], refs[27:33], refs[33], refs[34]
    moves = [
        (hidden.at[block(k, 128), :], held.at[block(k, 128), :], hidden_o.at[block(k, 128), :])
        for k in range(8)
    ] + list(zip(shards, parts, shards_o))
    for k, (src, mid, _) in enumerate(moves):
        pltpu.make_async_copy(src, mid, sem_in.at[k]).start()
    for k, size in enumerate(VECTOR_SIZES):
        vectors_o[k][...] = gvec[k, 0:size]
    loss_o[0] = loss[0, 0]
    for k, (src, mid, dst) in enumerate(moves):
        pltpu.make_async_copy(src, mid, sem_in.at[k]).wait()
        pltpu.make_async_copy(mid, dst, sem_out.at[k]).start()
    for k, (_, mid, dst) in enumerate(moves):
        pltpu.make_async_copy(mid, dst, sem_out.at[k]).wait()


def fused_device(hidden_in, seq_lengths, pos_index, pos_count, *masters):
    x = hidden_in.reshape(TOK, WIDTH)
    whole = pl.BlockSpec(memory_space=pltpu.VMEM)
    scalars = pl.BlockSpec(memory_space=pltpu.SMEM)
    away = pl.BlockSpec(memory_space=pl.ANY)
    shape = jax.ShapeDtypeStruct
    square = shape((24, 768), F32)
    shards = [square] * 4 + [shape((24, 3072), F32), shape((96, 768), F32)]
    pieces = len(PIECES)
    outs = pl.pallas_call(
        step_kernel,
        out_shape=[
            shape((1, 1), F32),
            shape((TOK, WIDTH), F32),
            shape((12, 2, SENT, SENT), BF),
            *shards,
            shape((16, 128), F32),
        ],
        in_specs=[scalars, away, whole, whole] + [away] * 6 + [whole] * 9,
        out_specs=[whole, away, away] + [whole] * 7,
        scratch_shapes=[
            pltpu.VMEM((WIDTH, INNER), BF),
            pltpu.VMEM((WIDTH, INNER), BF),
            pltpu.VMEM((INNER, WIDTH), BF),
            pltpu.VMEM((512, 128), F32),
            pltpu.VMEM((INNER, WIDTH), BF),
            pltpu.VMEM((SLOTS, 384, 768), BF),
            pltpu.VMEM((SLOTS, 2, 96, 384), BF),
            pltpu.VMEM((SLOTS, 2, 96, 768), BF),
            pltpu.VMEM((SLOTS, 3, 24, 768), BF),
            pltpu.VMEM((TOK, INNER), BF),
            pltpu.VMEM((TOK, INNER), BF),
            pltpu.VMEM((TOK, 2304), BF),
            pltpu.VMEM((TOK, WIDTH), BF),
            pltpu.VMEM((TOK, WIDTH), BF),
            pltpu.VMEM((TOK, WIDTH), BF),
            pltpu.VMEM((TOK, WIDTH), BF),
            pltpu.VMEM((TOK, WIDTH), F32),
            pltpu.VMEM((2, 2, SENT, SENT), BF),
            pltpu.VMEM((TOK, 1), F32),
            pltpu.VMEM((TOK, 1), F32),
            pltpu.VMEM((16, INNER), F32),
            pltpu.VMEM((16, INNER), F32),
            pltpu.VMEM((8, WIDTH), F32),
            pltpu.VMEM((8, WIDTH), F32),
            pltpu.VMEM((512, 128), BF),
            pltpu.VMEM((512, 128), F32),
            pltpu.VMEM((256, 128), F32),
            pltpu.VMEM((2, 32, 128), F32),
            pltpu.VMEM((2, 64, 128), F32),
            pltpu.VMEM((3, 16, 128), F32),
            pltpu.SemaphoreType.DMA((pieces, 6)),
            pltpu.SemaphoreType.DMA((pieces,)),
            pltpu.SemaphoreType.DMA((VEC + 1, 6)),
            pltpu.SemaphoreType.DMA((VEC + 1, 2)),
            pltpu.SemaphoreType.REGULAR((SLOTS,)),
            pltpu.SemaphoreType.DMA,
            pltpu.SemaphoreType.DMA,
            pltpu.SemaphoreType.DMA((2,)),
            pltpu.SemaphoreType.DMA((4,)),
            pltpu.SemaphoreType.DMA((10,)),
            pltpu.VMEM((TOK, WIDTH), BF),
        ],
        compiler_params=pltpu.CompilerParams(
            collective_id=0, has_side_effects=True, vmem_limit_bytes=VMEM_ALL
        ),
        name="train_step",
    )(seq_lengths.reshape(2), x, pos_index, pos_count, *masters)
    loss, hidden, grads = outs[0], outs[1], outs[3:]
    vectors = [shape((size,), F32) for size in VECTOR_SIZES]
    final = pl.pallas_call(
        emit_kernel,
        out_shape=[shape((TOK, WIDTH), F32), *shards, *vectors, shape((1,), F32)],
        in_specs=[away] * 7 + [whole, scalars],
        out_specs=[away] * 7 + [whole] * 9 + [scalars],
        scratch_shapes=[pltpu.VMEM((TOK, WIDTH), F32)]
        + [pltpu.VMEM(s.shape, F32) for s in shards]
        + [pltpu.SemaphoreType.DMA((14,)), pltpu.SemaphoreType.DMA((14,))],
        name="emit",
    )(hidden, *grads[:6], grads[6], loss)
    return (final[16].reshape(()), final[0].reshape(hidden_in.shape), *final[1:16])


def device_step(mesh):
    if mesh.shape["twin"] == 2 and mesh.shape["dp"] == 16:
        return fused_device
    return staged_device


def solution(mesh):
    in_specs = (
        P("twin", "dp", None, None),
        P("twin", "dp"),
        P(),
        P(),
        P(("twin", "dp"), None),
        P(("twin", "dp"), None),
        P(("twin", "dp"), None),
        P(("twin", "dp"), None),
        P(("twin", "dp"), None),
        P(("twin", "dp"), None),
        P(("twin", "dp")),
        P(("twin", "dp")),
        P(("twin", "dp")),
        P(("twin", "dp")),
        P(("twin", "dp")),
        P(("twin", "dp")),
        P(("twin", "dp")),
        P(("twin", "dp")),
        P(("twin", "dp")),
    )
    out_specs = (
        P(),
        P("twin", "dp", None, None),
        P(("twin", "dp"), None),
        P(("twin", "dp"), None),
        P(("twin", "dp"), None),
        P(("twin", "dp"), None),
        P(("twin", "dp"), None),
        P(("twin", "dp"), None),
        P(("twin", "dp")),
        P(("twin", "dp")),
        P(("twin", "dp")),
        P(("twin", "dp")),
        P(("twin", "dp")),
        P(("twin", "dp")),
        P(("twin", "dp")),
        P(("twin", "dp")),
        P(("twin", "dp")),
    )
    return jax.shard_map(
        device_step(mesh), mesh=mesh, in_specs=in_specs, out_specs=out_specs, check_vma=False
    )
```

profile of v0, /device:TPU:0, one launch (start us, length us, event | category | flops | bytes accessed | tf_op | source)
XLA Modules:
  0.0 188.9 jit_solution(873924333384114076)
XLA Ops:
  0.7 1.4 copy.36.refs_2_
  2.0 181.2 %train_step.1 = (f32[1,1]{1,0:T(1,128)}, f32[1024,768]{1,0:T(8,128)}, bf16[12,2,512,512]{3,2,1,0:T(8,128)(2,1)}, f32[24,768]{1,0:T(8,128)}, f32[24,768]{1,0:T(8,...) custom-call(s32[2]{0:T(128)} %bitcast.5, ...), custom_call_target="tpu_custom_call" | custom-call | tf_op jit(solution)/shard_map/train_step/pallas_call | solution.py:1222
  183.3 5.4 %emit.1 = (f32[1024,768]{1,0:T(8,128)}, f32[24,768]{1,0:T(8,128)}, f32[24,768]{1,0:T(8,128)}, f32[24,768]{1,0:T(8,128)}, f32[24,768]{1,0:T(8,128)}, /*index=5*/f...) custom-call(f32[1024,768]{1,0:T(8,128)} %get-tuple-element.43.refs_0, ...), custom_call_target="tpu_custom_call" | custom-call | tf_op jit(solution)/shard_map/emit/pallas_call | solution.py:1283
where the time goes:
time: 189 us
  Pallas kernels  187 us (99%)
    pallas_call x1, Pallas kernels, fused_device(): pl.pallas_call(step_kernel, out_shape=[shape((1, 1), F32), shape((TOK, WI...  181 us
    pallas_call x1, Pallas kernels, fused_device(): pl.pallas_call(emit_kernel, out_shape=[shape((TOK, WIDTH), F32), *shards,...  5.42 us

commit v1 on v0

--- a/solution.py
+++ b/solution.py
@@ -338,6 +338,8 @@
     + [(1, 24, 768 * j, 768) for j in range(4)]
     + [(2, 96, 256 * j, 256) for j in range(3)]
 )
+LATE = ()
+EARLY = 13
 GRADS = (
     [(96, 24 * j, 0, 768) for j in range(4)]
     + [(24, 768 * j, 0, 768) for j in range(4)]
@@ -347,60 +349,62 @@
 VEC = len(GRADS)
 
 AHEAD = 5
-FORWARD = {'attend0': {0: ('g2', 'k5', 'a10'), 1: ('f2',), 2: ('g3',), 3: ('k7', 'a12')},
- 'attend1': {0: ('k8',), 1: ('g4',), 2: ('i6', 'k9', 'f4')},
- 'attend2': {0: ('k10',), 1: ('g5',), 3: ('f5', 'i8', 'k11', 'g6')},
- 'exp0': {0: ('k12',), 1: ('g7',), 4: ('f7',), 5: ('i10',)},
- 'exp1': {1: ('g8',), 4: ('f8',), 5: ('i11',)},
- 'exp2': {1: ('g9',), 4: ('f9',), 5: ('i12',)},
- 'exp3': {2: ('g10',), 5: ('f10', 'g11')},
- 'mix': {3: ('f6', 'i9')},
+FORWARD = {'attend0': {0: ('g2', 'k5', 'a10'),
+             1: ('k6', 'a11', 'i4'),
+             2: ('g3',),
+             3: ('k7', 'a12')},
+ 'attend1': {0: ('k8',), 1: ('i6',), 2: ('k9', 'g4')},
+ 'attend2': {0: ('g5',), 2: ('f5', 'i8', 'k11'), 3: ('g6',)},
+ 'exp0': {0: ('g7',), 4: ('f7', 'i10')},
+ 'exp1': {0: ('g8',), 4: ('f8', 'i11')},
+ 'exp2': {2: ('i12',), 4: ('g9',)},
+ 'exp3': {-1: ('g10', 'f9'), 2: ('f10', 'g11'), 5: ('g12',)},
+ 'mix': {1: ('k12', 'i9'), 3: ('f6',)},
  'proj0': {-1: ('f1',), 1: ('i3',)},
- 'proj1': {-1: ('f3',), 2: ('i5',)},
- 'proj2': {4: ('i7',)},
- 'projh': {0: ('i4',), 1: ('k6', 'a11')},
- 'shr1': {-1: ('g12', 'f11')},
+ 'proj1': {-1: ('i5', 'f3')},
+ 'proj2': {-1: ('i7', 'f4'), 1: ('k10',)},
+ 'projh': {-1: ('f2',)},
+ 'shr0': {0: ('f11',)},
  'shr2': {-1: ('f12',)},
  'vec': {-1: ('k0',
               'a5',
               'k1',
               'a6',
-              'i0',
               'k2',
               'a7',
+              'i0',
               'i1',
-              'g0',
               'k3',
               'a8',
               'i2',
-              'f0'),
-         5: ('g1',),
-         7: ('k4', 'a9')}}
-BACKWARD = {'actb': {2: ('c0', 'r0'),
-          3: ('c1', 'r1'),
-          4: ('c2', 'r2', 'c3', 'r3'),
-          6: ('d0',),
-          8: ('d1',),
-          10: ('d2',)},
- 'attb0': {0: ('c8', 's5', 'r8'), 2: ('f4', 's6'), 3: ('s7', 'f5')},
- 'attb1': {1: ('f6', 's8', 'c9', 'r9'), 2: ('f7',), 3: ('d9',)},
- 'attb2': {0: ('f8',), 1: ('s9', 'c10', 'r10'), 2: ('c11', 'r11'), 3: ('d10',)},
- 'expg0': {0: ('d3',)},
- 'expg1': {1: ('s0',)},
- 'expg2': {0: ('c4', 'r4'), 2: ('s1', 'c5', 'r5')},
- 'expg3': {2: ('s2',)},
- 'firstb': {0: ('r6',),
-            1: ('f1', 's3', 'd4', 'c7', 'r7'),
-            2: ('f2', 'd5', 'd6')},
- 'inb': {0: ('c12', 's10', 'r12', 'c13', 'r13'),
-         1: ('s11',),
-         2: ('d12', 'd13')},
- 'ing0': {0: ('d8',)},
- 'ingh1': {0: ('f9',), 1: ('d11',)},
- 'mixb': {0: ('f3', 'd7')},
- 'mixg': {1: ('s4',)},
- 'st7': {-1: ('c6', 'f0')},
- 'tail': {-1: ('f10', 's12', 's13', 'f11', 'f12', 'f13')}}
+              'g0',
+              'k4',
+              'a9',
+              'g1',
+              'f0')}}
+BACKWARD = {'actb': {3: ('c0', 'r0'),
+          4: ('c1', 'r1', 'c2', 'r2'),
+          5: ('c3', 'r3'),
+          8: ('d0',),
+          10: ('d1',)},
+ 'attb0': {0: ('s5', 'c8', 'r8'), 1: ('d7',), 2: ('s6',), 3: ('f4', 'd8')},
+ 'attb1': {1: ('f6', 's8', 'c9', 'r9'), 3: ('f7',)},
+ 'attb2': {0: ('f8',), 1: ('c10', 'r10'), 3: ('d10', 'c11', 'r11')},
+ 'expg0': {0: ('d2',), 2: ('d3',)},
+ 'expg2': {0: ('s0',), 1: ('c4', 'r4')},
+ 'expg3': {0: ('c5', 's1', 'r5')},
+ 'firstb': {0: ('s3',), 1: ('f1', 'd4', 'd5', 'c7', 'r7'), 2: ('f2', 'd6')},
+ 'inb': {0: ('c12', 'r12'),
+         1: ('s10', 'c13', 'r13'),
+         2: ('d11',),
+         4: ('d12', 'd13')},
+ 'ing0': {2: ('f5', 's7')},
+ 'ing1': {0: ('d9',)},
+ 'ingh0': {0: ('s9',)},
+ 'mixb': {0: ('f3', 's4')},
+ 'st7': {-1: ('c6', 'r6', 's2', 'f0')},
+ 'tail': {-1: ('s11', 's12', 'f10', 's13', 'f11', 'f12', 'f13')},
+ 'tiles': {2: ('f9',)}}
 
 
 def coords():
@@ -469,41 +473,65 @@
     def start(self, p):
         t, z, y, c = self.at
         own = self.rows(p, flat(t, z, y, c))
+        self.along_z(p, own)
+        if p < EARLY or p in LATE:
+            self.across(p, own)
+
+    def across(self, p, part):
+        t, z, y, c = self.at
+        self.put(p, part, dev(1 - t, z, y, c), 1)
+        self.put(p, part, dev(t, z, 1 - y, c), 2)
+        self.put(p, part, dev(t, z, y, 1 - c), 5)
+
+    def along_z(self, p, part):
+        t, z, y, c = self.at
         for k in (1, 2, 3):
-            self.put(p, own, dev(t, (z + k) % 4, y, c), 0)
-        self.put(p, own, dev(1 - t, z, y, c), 1)
-        self.put(p, own, dev(t, z, 1 - y, c), 2)
-        self.put(p, own, dev(t, z, y, 1 - c), 5)
+            self.put(p, part, dev(t, (z + k) % 4, y, c), 0)
 
     def column(self, p):
         t, z, y, c = self.at
+        if p in LATE:
+            self.wait(p, 0, 12)
+            for k in (1, 2, 3):
+                for tt in range(2):
+                    for yy in range(2):
+                        part = self.rows(p, flat(tt, (z + k) % 4, yy, c))
+                        self.put(p, part, dev(t, z, y, 1 - c), 5)
+            return
         self.wait(p, 0, 3)
-        for k in (1, 2, 3):
-            part = self.rows(p, flat(t, (z + k) % 4, y, c))
-            self.put(p, part, dev(1 - t, z, y, c), 1)
-            self.put(p, part, dev(t, z, 1 - y, c), 2)
-            self.put(p, part, dev(t, z, y, 1 - c), 5)
+        for k in range(1 if p < EARLY else 0, 4):
+            self.across(p, self.rows(p, flat(t, (z + k) % 4, y, c)))
 
     def sides(self, p):
         t, z, y, c = self.at
-        self.wait(p, 1, 4)
-        owners = [flat(1 - t, k, y, c) for k in range(4)]
+        steps = [z] if p in LATE else range(4)
+        self.wait(p, 1, len(steps))
+        owners = [flat(1 - t, k, y, c) for k in steps]
         for part in self.halves(p, owners, 0):
             self.put(p, part, dev(t, z, 1 - y, c), 4)
         for owner in owners:
             self.put(p, self.rows(p, owner), dev(t, z, y, 1 - c), 5)
-        self.wait(p, 2, 4)
-        owners = [flat(t, k, 1 - y, c) for k in range(4)]
+            if p in LATE:
+                self.along_z(p, self.rows(p, owner))
+        self.wait(p, 2, len(steps))
+        owners = [flat(t, k, 1 - y, c) for k in steps]
         for part in self.halves(p, owners, 1):
             self.put(p, part, dev(1 - t, z, y, c), 3)
         for owner in owners:
             self.put(p, self.rows(p, owner), dev(t, z, y, 1 - c), 5)
+            if p in LATE:
+                self.along_z(p, self.rows(p, owner))
 
     def diagonal(self, p):
         t, z, y, c = self.at
-        owners = [flat(1 - t, k, 1 - y, c) for k in range(4)]
+        owners = [flat(1 - t, k, 1 - y, c) for k in ([z] if p in LATE else range(4))]
         for group, half in ((3, 1), (4, 0)):
-            self.wait(p, group, 2)
+            if p in LATE:
+                part = self.halves(p, owners, half)[0]
+                wait_bytes(part, self.recv.at[p, group])
+                self.along_z(p, part)
+            else:
+                self.wait(p, group, 2)
             for part in self.halves(p, owners, half):
                 self.put(p, part, dev(t, z, y, 1 - c), 5)
 
@@ -710,14 +738,22 @@
     return owner, n - owner * size
 
 
-def vector_row(vec, k):
-    size = VECTOR_SIZES[k]
-    width = 32 * size
-    owner, place = owner_of(iota((1, width), 1), size)
-    shards = vec[pl.ds(k, 32, stride=16), :].astype(BF)
-    pick = jnp.where(iota((128, width), 0) == place, 1.0, 0.0).astype(BF)
-    spreaded = dot(shards, pick)
-    return jnp.sum(jnp.where(iota((32, width), 0) == owner, spreaded, 0.0), axis=0, keepdims=True)
+def picks(size, first):
+    width = 256
+    owner, place = owner_of(first + iota((1, width), 1), size)
+    return (
+        jnp.where(iota((128, width), 0) == place, 1.0, 0.0).astype(BF),
+        jnp.where(iota((32, width), 0) == owner, 1.0, 0.0).astype(BF),
+    )
+
+
+def vector_rows(vec, par, names, pick, mine):
+    width = pick.shape[1]
+    shards = [vec[pl.ds(k, 32, stride=16), :].astype(BF) for k in names]
+    spreaded = dot(jnp.concatenate(shards, axis=0), pick)
+    for i, k in enumerate(names):
+        part = spreaded[32 * i : 32 * i + 32] * mine.astype(F32)
+        par[k : k + 1, 0:width] = jnp.sum(part, axis=0, keepdims=True)
 
 
 def vector_tiles(row, k):
@@ -742,7 +778,25 @@
     return center * scale, scale
 
 
-def contrast(pool, pos, cnt, dpool, own):
+def targets(pos, cnt):
+    goals = []
+    eye16 = iota((16, 16), 0) == iota((16, 16), 1)
+    eye32 = jnp.where(iota((32, 32), 0) == iota((32, 32), 1), 1.0, 0.0).astype(BF)
+    for m in range(MICRO):
+        number = cnt[m : m + 1, :]
+        hits = jnp.zeros((32, 16), F32)
+        for k in range(6):
+            hit = (pos[k, m : m + 1, :] + 16 == iota((32, 16), 0)) & (k < number)
+            hits = hits + jnp.where(hit, 1.0, 0.0)
+        hits = dot_lt(hits.astype(BF), eye32)
+        number = jnp.sum(jnp.where(eye16, number, 0), axis=1, keepdims=True)
+        goals.append(
+            jnp.concatenate([hits / number.astype(F32), jnp.zeros((16, 32), F32)], axis=0)
+        )
+    return goals
+
+
+def contrast(pool, goals, dpool, own):
     total = jnp.zeros((1, 1), F32)
     row, col = iota((32, 32), 0), iota((32, 32), 1)
     valid = (row < 16) & (col >= 16)
@@ -760,13 +814,7 @@
         terms = jnp.where(valid, jnp.exp(jnp.minimum(sims - top, 0.0)), 0.0)
         row_sum = jnp.where(row[:, :1] < 16, jnp.sum(terms, axis=1, keepdims=True), 1.0)
         logs = jnp.where(row[:, :1] < 16, top + jnp.log(row_sum), 0.0)
-        hits = jnp.zeros((16, 32), F32)
-        eye16 = iota((16, 16), 0) == iota((16, 16), 1)
-        number = jnp.sum(jnp.where(eye16, cnt[m : m + 1, :], 0), axis=1, keepdims=True)
-        for k in range(6):
-            hit = (pos[m, :, k : k + 1] + 16 == iota((16, 32), 1)) & (k < number)
-            hits = hits + jnp.where(hit, 1.0, 0.0)
-        target = jnp.concatenate([hits / number.astype(F32), jnp.zeros((16, 32), F32)], axis=0)
+        target = goals[m]
         loss = logs - jnp.sum(target * sims, axis=1, keepdims=True)
         total = total + jnp.sum(jnp.where(row[:, :1] < 16, loss, 0.0), axis=0, keepdims=True)
         grad = (terms / row_sum - target) * static_scale
@@ -797,10 +845,10 @@
     mvec = refs[10:19]
     (loss, hidden, probs, gq, gk, gv, gm, ge, gs, gvec) = refs[19:29]
     (wa, we, ws, vec, grad, rc, rd, rs, rz, act, gp, qkv, mixed, nb, n1, n2) = refs[29:45]
-    (f1, pbuf, r1, r2, par, pgrad, nbar, dpool, pool, poolf) = refs[45:55]
-    (vc, vd, vs, vz) = refs[55:59]
-    vgrad = vec
-    (g_recv, g_sent, s_recv, s_sent, free, pool_recv, pool_sent, p_sem, h_sem, in_sem, x) = refs[59:]
+    (f1, pbuf, r1, r2, par, pgrad, nbar, dpool, pool) = refs[45:54]
+    (vc, vd, vs, vz) = refs[54:58]
+    vgrad = poolf = vec
+    (g_recv, g_sent, s_recv, s_sent, free, pool_recv, pool_sent, p_sem, h_sem, in_sem, x) = refs[58:]
     t, z, y, c = coords()
     own = flat(t, z, y, c)
     gather = Gather((wa, we, ws, vec), g_recv, g_sent)
@@ -840,6 +888,8 @@
     for j in range(4):
         we[here24, 768 * j : 768 * j + 768] = f1[192 + 24 * j : 216 + 24 * j, :].astype(BF)
     ws[pl.ds(pl.multiple_of(own * 96, 8), 96), :] = f1[96:192, :].astype(BF)
+    for p in range(5, AHEAD):
+        gather.start(p)
 
     def planned(name):
         ticks = ticks_of(FORWARD, name, gather.table())
@@ -847,12 +897,20 @@
             part()
         return ticks
 
+    for ref, size, blocks in ((gp, 24, 3), (act, 96, 12)):
+
+        def pick(i, ref=ref, size=size):
+            ref[0:128, block(i, 256)], ref[128:160, block(i, 256)] = picks(size, 256 * i)
+
+        loop(blocks, pick)
     ticks = planned("vec")
-    for k, size in enumerate(VECTOR_SIZES):
-        par[k : k + 1, 0 : 32 * size] = vector_row(vec, k)
-        for part in ticks.get(k, ()):
-            part()
-
+    small = [k for k in range(9) if k != EB]
+    vector_rows(vec, par, small, gp[0:128, 0:768], gp[128:160, 0:768])
+    for part in ticks.get(0, ()):
+        part()
+    vector_rows(vec, par, [EB], act[0:128, :], act[128:160, :])
+    for part in ticks.get(1, ()):
+        part()
     for g in range(6):
         lanes, first = slice(128 * g, 128 * g + 128), 384 * g
         par[9:10, first : first + 128] = par[QB : QB + 1, lanes] * HDIM ** (-0.5)
@@ -993,9 +1051,10 @@
     lax.fori_loop(1, 32, spread_pool, 0)
     for p in range(len(PIECES)):
         gather.drain(p)
+    goals = targets(pos, cnt)
     wait_bytes(pool.at[pl.ds(0, 496), :], pool_recv)
     poolf[...] = pool[...].astype(F32)
-    loss[...] = contrast(poolf, pos, cnt, dpool, own) / (MICRO * 16)
+    loss[...] = contrast(poolf, goals, dpool, own) / (MICRO * 16)
     wait_bytes(pool.at[pl.ds(0, 496), :], pool_sent)
 
     def store(p, total):
@@ -1170,23 +1229,27 @@
                 pgrad[k : k + 1, lanes] = jnp.sum(
                     act[:, col : col + 128].astype(F32), axis=0, keepdims=True
                 )
+    ticks = planned("tiles")
     for k in range(9):
         tiles = vector_tiles(pgrad[k : k + 1, 0 : 32 * VECTOR_SIZES[k]], k)
         vgrad[pl.ds(k, 32, stride=16), :] = tiles
+        if k % 3 == 2:
+            for part in ticks.get(k // 3, ()):
+                part()
     scatter.start(VEC)
 
     def put_hidden(i):
-        rows = block(i, 256)
-        return pltpu.make_async_copy(f1.at[rows, :], hidden.at[rows, :], h_sem.at[i])
+        at = (block(i // 3, 512), block(i % 3, 256))
+        return pltpu.make_async_copy(f1.at[at], hidden.at[at], h_sem.at[i])
 
     def input_back(i):
-        rows = block(i, 256)
-        f1[rows, :] = f1[rows, :] + dot_rt(act[rows, 0:2304], wa[:, 0:2304])
+        rows, cols = block(i // 3, 512), block(i % 3, 256)
+        f1[rows, cols] = f1[rows, cols] + dot_rt(act[rows, 0:2304], wa[cols, 0:2304])
         put_hidden(i).start()
 
-    loop(4, input_back, planned("inb"))
+    loop(6, input_back, planned("inb"))
     planned("tail")
-    for i in range(4):
+    for i in range(6):
         put_hidden(i).wait()
 
 
@@ -1256,7 +1319,6 @@
             pltpu.VMEM((8, WIDTH), F32),
             pltpu.VMEM((8, WIDTH), F32),
             pltpu.VMEM((512, 128), BF),
-            pltpu.VMEM((512, 128), F32),
             pltpu.VMEM((256, 128), F32),
             pltpu.VMEM((2, 32, 128), F32),
             pltpu.VMEM((2, 64, 128), F32),
@@ -1269,7 +1331,7 @@
             pltpu.SemaphoreType.DMA,
             pltpu.SemaphoreType.DMA,
             pltpu.SemaphoreType.DMA((2,)),
-            pltpu.SemaphoreType.DMA((4,)),
+            pltpu.SemaphoreType.DMA((6,)),
             pltpu.SemaphoreType.DMA((10,)),
             pltpu.VMEM((TOK, WIDTH), BF),
         ],
@@ -1277,7 +1339,7 @@
             collective_id=0, has_side_effects=True, vmem_limit_bytes=VMEM_ALL
         ),
         name="train_step",
-    )(seq_lengths.reshape(2), x, pos_index, pos_count, *masters)
+    )(seq_lengths.reshape(2), x, jnp.transpose(pos_index, (2, 0, 1)), pos_count, *masters)
     loss, hidden, grads = outs[0], outs[1], outs[3:]
     vectors = [shape((size,), F32) for size in VECTOR_SIZES]
     final = pl.pallas_call(

time: 189 us -> 188 us (level)
  no operation moved by 1% of the time
where the time goes in v1:
time: 188 us; the launch traced here: 187 us
  Pallas kernels  187 us (99%)
    pallas_call x1, Pallas kernels, fused_device(): pl.pallas_call(step_kernel, out_shape=[shape((1, 1), F32), shape((TOK, WI...  181 us
    pallas_call x1, Pallas kernels, fused_device(): pl.pallas_call(emit_kernel, out_shape=[shape((TOK, WIDTH), F32), *shards,...  5.42 us

profile of v1, /device:TPU:0, one launch (start us, length us, event | category | flops | bytes accessed | tf_op | source)
XLA Modules:
  0.0 187.4 jit_solution(13293437968307546439)
XLA Ops:
  0.7 181.1 %train_step.1 = (f32[1,1]{1,0:T(1,128)}, f32[1024,768]{1,0:T(8,128)}, bf16[12,2,512,512]{3,2,1,0:T(8,128)(2,1)}, f32[24,768]{1,0:T(8,128)}, f32[24,768]{1,0:T(8,...) custom-call(s32[2]{0:T(128)} %bitcast.7, ...), custom_call_target="tpu_custom_call" | custom-call | tf_op jit(solution)/shard_map/train_step/pallas_call | solution.py:1285
  181.8 5.4 %emit.1 = (f32[1024,768]{1,0:T(8,128)}, f32[24,768]{1,0:T(8,128)}, f32[24,768]{1,0:T(8,128)}, f32[24,768]{1,0:T(8,128)}, f32[24,768]{1,0:T(8,128)}, /*index=5*/f...) custom-call(f32[1024,768]{1,0:T(8,128)} %get-tuple-element.43.refs_0, ...), custom_call_target="tpu_custom_call" | custom-call | tf_op jit(solution)/shard_map/emit/pallas_call | solution.py:1345
